TPU v7x, 32 devices: a whole 2x2x4 slice. The times are simulated.
32 devices in a mesh: row: 4 (over y, x), col: 8 (over z, core).
Axes of the slice: x: 2, y: 2, z: 4, core: 2. Of those that a mesh axis runs over, the one named last changes fastest.
Arguments:
- vorticity: float32 [3, 128, 128, 128], P(None, 'row', 'col'), may hold values from -18.1 to 18.1
- scalar: float32 [256, 256, 256], P('row', 'col'), may hold values from -6 to 6
Outputs:
- advected: float32 [256, 256, 256], P('row', 'col')
All inputs are finite; a program needn't handle non-finite values. Where the computation divides by a largest or mean magnitude, that divisor is 1e-20 or more.
Results may differ from a plain program's by a relative error of at most 0.0003.
Values sent between devices are 32-bit elements; how exact they have to be, the bound alone decides.
A program may use at most 128 MiB of HBM per device.

v0:
```python
import math

import jax
import jax.numpy as jnp
from jax import lax
from jax.sharding import PartitionSpec as P

COURANT = 0.9
EPSILON = 1e-06
HIGHEST = lax.Precision.HIGHEST


def with_halo(cells, sides, width):
    for axis, dim in sides:
        count = lax.axis_size(axis)
        head = lax.slice_in_dim(cells, 0, width, axis=dim)
        tail = lax.slice_in_dim(cells, cells.shape[dim] - width, cells.shape[dim], axis=dim)
        cells = jnp.concatenate(
            [
                lax.ppermute(tail, axis, [(i, (i + 1) % count) for i in range(count)]),
                cells,
                lax.ppermute(head, axis, [((i + 1) % count, i) for i in range(count)]),
            ],
            axis=dim,
        )
    return cells


def kernel_weight(distance):
    radius = jnp.abs(distance)
    inner_lobe = (
        -(radius - 1.0)
        * ((((25.0 * radius - 38.0) * radius - 3.0) * radius + 12.0) * radius + 12.0)
        / 12.0
    )
    middle_lobe = (
        (radius - 1.0)
        * (radius - 2.0)
        * (((25.0 * radius - 114.0) * radius + 153.0) * radius - 48.0)
        / 24.0
    )
    outer_cube = (radius - 3.0) * (radius - 3.0) * (radius - 3.0)
    outer_lobe = -(radius - 2.0) * outer_cube * (5.0 * radius - 8.0) / 24.0
    return jnp.where(
        radius < 1.0,
        inner_lobe,
        jnp.where(radius < 2.0, middle_lobe, jnp.where(radius < 3.0, outer_lobe, 0.0)),
    )


def tables(length):
    indices = jnp.arange(length, dtype=jnp.int32)
    product = indices[:, None] * indices[None, :] % length
    angle = product.astype(jnp.float32) * (2.0 * math.pi / length)
    return (jnp.cos(angle), jnp.sin(angle))


def rotate(complex_pair, formula, cosine, sine, direction):
    real_cos = jnp.einsum(formula, complex_pair[0], cosine, precision=HIGHEST)
    real_sin = jnp.einsum(formula, complex_pair[0], sine, precision=HIGHEST)
    imag_cos = jnp.einsum(formula, complex_pair[1], cosine, precision=HIGHEST)
    imag_sin = jnp.einsum(formula, complex_pair[1], sine, precision=HIGHEST)
    return jnp.stack([real_cos - direction * imag_sin, imag_cos + direction * real_sin])


def wavenumber(start, count, length):
    indices = start + jnp.arange(count, dtype=jnp.int32)
    waves = jnp.where(indices < length // 2, indices, indices - length).astype(jnp.float32)
    return (waves, indices == length // 2)


def induce(spectrum, xwaves, ywaves, zwaves, banned, inverse_cube):
    wave_sq = xwaves * xwaves + ywaves * ywaves + zwaves * zwaves
    keep = (wave_sq > 0.0) & jnp.logical_not(banned)
    factor = jnp.where(keep, 1.0 / jnp.maximum(wave_sq, 1.0), 0.0) * inverse_cube
    crosses = []
    for part_index in range(2):
        omega = spectrum[part_index]
        crosses.append(
            jnp.stack(
                [
                    ywaves * omega[2] - zwaves * omega[1],
                    zwaves * omega[0] - xwaves * omega[2],
                    xwaves * omega[1] - ywaves * omega[0],
                ]
            )
        )
    return jnp.stack([-crosses[1] * factor, crosses[0] * factor])


def merged_shape(lower, grid_axis):
    shape = list(lower.shape)
    shape[grid_axis] = 2 * shape[grid_axis]
    return shape


def refine_roll(coarse, grid_axis):
    lower = 0.75 * coarse + 0.25 * jnp.roll(coarse, 1, grid_axis)
    upper = 0.75 * coarse + 0.25 * jnp.roll(coarse, -1, grid_axis)
    return jnp.stack([lower, upper], axis=grid_axis + 1).reshape(merged_shape(lower, grid_axis))


def refine_rim(coarse, grid_axis):
    length = coarse.shape[grid_axis]
    inner = lax.slice_in_dim(coarse, 1, length - 1, axis=grid_axis)
    below = lax.slice_in_dim(coarse, 0, length - 2, axis=grid_axis)
    above = lax.slice_in_dim(coarse, 2, length, axis=grid_axis)
    lower = 0.75 * inner + 0.25 * below
    upper = 0.75 * inner + 0.25 * above
    return jnp.stack([lower, upper], axis=grid_axis + 1).reshape(merged_shape(lower, grid_axis))


def remesh_roll(field, displace, grid_axis):
    summed = jnp.zeros(field.shape, jnp.float32)
    for offset in range(-3, 4):
        summed = summed + jnp.roll(field, offset, grid_axis) * kernel_weight(
            offset - jnp.roll(displace, offset, grid_axis)
        )
    return summed


def remesh_rim(field_ext, displace_ext, grid_axis, count):
    shape = list(field_ext.shape)
    shape[grid_axis] = count
    summed = jnp.zeros(shape, jnp.float32)
    for offset in range(-3, 4):
        begin = 3 - offset
        values = lax.slice_in_dim(field_ext, begin, begin + count, axis=grid_axis)
        moved = lax.slice_in_dim(displace_ext, begin, begin + count, axis=grid_axis)
        summed = summed + values * kernel_weight(offset - moved)
    return summed


def shards(vorticity, scalar):
    coarse_n = vorticity.shape[3]
    cos_full, sin_full = tables(coarse_n)
    mode_count = coarse_n // 2
    weights = jnp.where(jnp.arange(mode_count) == 0, 1.0, 2.0).astype(jnp.float32)
    cos_fwd = cos_full[:, :mode_count]
    sin_fwd = sin_full[:, :mode_count]
    cos_back = cos_full[:mode_count, :] * weights[:, None]
    sin_back = sin_full[:mode_count, :] * weights[:, None]
    forward = jnp.stack(
        [
            jnp.einsum("cyzx,xk->cyzk", vorticity, cos_fwd, precision=HIGHEST),
            -jnp.einsum("cyzx,xk->cyzk", vorticity, sin_fwd, precision=HIGHEST),
        ]
    )
    spectrum = rotate(
        lax.all_to_all(forward, "row", split_axis=4, concat_axis=2, tiled=True),
        "cyzk,yq->czkq",
        cos_full,
        sin_full,
        -1.0,
    )
    spectrum = rotate(
        lax.all_to_all(spectrum, "col", split_axis=4, concat_axis=2, tiled=True),
        "czkq,zw->ckqw",
        cos_full,
        sin_full,
        -1.0,
    )
    first_count = spectrum.shape[2]
    second_count = spectrum.shape[3]
    xwaves, xnyquist = wavenumber(lax.axis_index("row") * first_count, first_count, coarse_n)
    ywaves, ynyquist = wavenumber(lax.axis_index("col") * second_count, second_count, coarse_n)
    zwaves, znyquist = wavenumber(0, coarse_n, coarse_n)
    banned = xnyquist[:, None, None] | ynyquist[None, :, None] | znyquist[None, None, :]
    inverse_cube = 1.0 / (coarse_n * coarse_n * coarse_n)
    velocity_hat = induce(
        spectrum,
        xwaves[:, None, None],
        ywaves[None, :, None],
        zwaves[None, None, :],
        banned,
        inverse_cube,
    )
    inverse_z = rotate(velocity_hat, "ckqw,wz->ckqz", cos_full, sin_full, 1.0)
    mixed = rotate(
        lax.all_to_all(inverse_z, "col", split_axis=4, concat_axis=3, tiled=True),
        "ckqz,qy->ckzy",
        cos_full,
        sin_full,
        1.0,
    )
    block = lax.all_to_all(mixed, "row", split_axis=4, concat_axis=2, tiled=True)
    velocity = jnp.einsum("ckzy,kx->cyzx", block[0], cos_back, precision=HIGHEST) - jnp.einsum(
        "ckzy,kx->cyzx", block[1], sin_back, precision=HIGHEST
    )
    velocity_peak = lax.pmax(jnp.max(jnp.abs(velocity)), ("row", "col"))
    courant_scale = COURANT / (velocity_peak + EPSILON)
    fine_rows = scalar.shape[0]
    fine_cols = scalar.shape[1]
    rimmed = with_halo(velocity, (("row", 1), ("col", 2)), 1)
    displaced = refine_rim(refine_rim(refine_roll(rimmed, 3), 1), 2) * courant_scale
    swept = remesh_roll(scalar, displaced[0], 2)
    rows_input = jnp.stack([swept, displaced[1]])
    rows_ext = with_halo(rows_input, (("row", 1),), 3)
    ymoved = rows_ext[1]
    swept = remesh_rim(rows_ext[0], ymoved, 0, fine_rows)
    cols_input = jnp.stack([swept, displaced[2]])
    cols_ext = with_halo(cols_input, (("col", 2),), 3)
    zmoved = cols_ext[1]
    return remesh_rim(cols_ext[0], zmoved, 1, fine_cols)


def solution(mesh):
    in_specs = (P(None, "row", "col", None), P("row", "col", None))
    out_specs = P("row", "col", None)
    return jax.shard_map(shards, mesh=mesh, in_specs=in_specs, out_specs=out_specs, check_vma=False)
```

profile of v0, /device:TPU:0, one launch (start us, length us, event | category | flops | bytes accessed | tf_op | source)
XLA Modules:
  0.0 477.7 jit_solution(8644423327381944516)
XLA Ops:
  3.1 2.5 copy.292
  5.6 3.4 reshape.296
  9.0 16.6 %all_to_all.60 = f32[4,1,49152]{2,1,0:T(1,128)S(1)} all-to-all(f32[4,1,49152]{2,1,0:T(1,128)S(1)} %reshape.296), channel_id=1, replica_groups=mesh['row'=4,'col'=8] {'row'}, dimensions={0} | all-to-all | bytes 1572864 | tf_op jit(solution)/shard_map/all_to_all | solution.py:150
  26.2 3.0 reduce
  29.1 2.7 reshape.297
  31.9 3.7 copy.293
  37.8 2.1 squeeze.23
  42.4 2.1 squeeze.22
  46.8 6.5 %copy.296 = f32[2,3,16,16,128]{3,2,1,0,4:T(8,128)} copy(f32[2,3,16,16,128]{4,3,2,1,0:T(8,128)S(1)} %pad_maximum_fusion.7) | data formatting | bytes 1572864 | tf_op jit(solution)/shard_map/stack | solution.py:63
  53.3 5.5 %reshape.298 = f32[8,1,24576]{2,1,0:T(1,128)} reshape(f32[128,2,3,16,16]{4,3,2,1,0:T(8,128)} %bitcast.181) | data formatting | bytes 1572864
  58.8 4.9 %all-to-all-start.1 = ((f32[8,1,24576]{2,1,0:T(1,128)}), f32[8,1,24576]{2,1,0:T(1,128)S(1)}, u32[]{:S(2)}, u32[]{:S(2)}) async-start(f32[8,1,24576]{2,1,0:T(1,128)} %reshape.298), calls=%async_computation.1 | async-start | bytes 1572864 | tf_op jit(solution)/shard_map/all_to_all | solution.py:157
  64.0 20.6 %all-to-all-done.1 = f32[8,1,24576]{2,1,0:T(1,128)S(1)} async-done(((f32[8,1,24576]{2,1,0:T(1,128)}), f32[8,1,24576]{2,1,0:T(1,128)S(1)}, u32[]{:S(2)}, u32[]{:S(2)}) %all-to-all-start.1) | async-done | bytes 786464 | tf_op jit(solution)/shard_map/all_to_all | solution.py:157
  84.6 2.6 reduce.1
  87.2 4.8 %reshape.299 = f32[128,2,3,16,16]{4,3,2,1,0:T(8,128)} reshape(f32[8,24576]{1,0:T(8,128)S(1)} %reduce.1) | data formatting | bytes 1572864
  92.0 8.0 %copy.297 = f32[2,3,16,16,8,16]{2,4,5,3,1,0:T(8,128)} copy(f32[2,3,16,16,8,16]{3,2,1,0,5,4:T(8,128)} %bitcast.182) | data formatting | bytes 1572864 | tf_op jit(solution)/shard_map/all_to_all | solution.py:157
  100.0 6.3 %fusion.342 = (f32[1,3,8,16,16,16]{3,2,5,4,1,0:T(8,128)}, f32[1,3,8,16,16,16]{3,2,5,4,1,0:T(8,128)}) fusion(f32[2,3,8,16,16,16]{3,2,5,4,1,0:T(8,128)} %bitcast.179), kind=kLoop, calls=%fused_computation.442 | loop fusion | bytes 1572864 | tf_op jit(solution)/shard_map/slice | solution.py:60
  106.3 2.4 squeeze.25
  109.4 2.6 squeeze.24
  117.3 6.0 %copy.298 = f32[2,3,16,16,128]{3,2,1,0,4:T(8,128)} copy(f32[2,3,16,16,128]{4,3,2,1,0:T(8,128)S(1)} %pad_maximum_fusion.8) | data formatting | bytes 1572864 | tf_op jit(solution)/shard_map/stack | solution.py:63
  123.4 5.6 %reshape.300 = f32[8,1,24576]{2,1,0:T(1,128)} reshape(f32[128,2,3,16,16]{4,3,2,1,0:T(8,128)} %bitcast.183) | data formatting | bytes 1572864
  129.0 4.4 all-to-all-start.2
  133.4 2.9 fusion.352
  136.3 2.9 fusion.354
  139.1 15.2 %all-to-all-done.2 = f32[8,1,24576]{2,1,0:T(1,128)} async-done(((f32[8,1,24576]{2,1,0:T(1,128)}), f32[8,1,24576]{2,1,0:T(1,128)}, u32[]{:S(2)}, u32[]{:S(2)}) %all-to-all-start.2) | async-done | bytes 786464 | tf_op jit(solution)/shard_map/all_to_all | solution.py:180
  154.4 3.7 reduce.2
  158.1 4.8 reshape.301
  162.8 6.4 %copy.353 = f32[2,3,16,16,8,16]{3,4,5,2,1,0:T(8,128)S(1)} copy(f32[2,3,16,16,8,16]{3,2,1,0,5,4:T(8,128)} %bitcast.184) | data formatting | bytes 1572864 | tf_op jit(solution)/shard_map/all_to_all | solution.py:180
  169.3 3.1 fusion.341
  172.4 2.4 squeeze.26
  175.5 2.9 squeeze.27
  180.6 6.0 %copy.300 = f32[2,3,16,16,128]{3,2,1,0,4:T(8,128)} copy(f32[2,3,16,16,128]{4,3,2,1,0:T(8,128)S(1)} %pad_maximum_fusion.9) | data formatting | bytes 1572864 | tf_op jit(solution)/shard_map/stack | solution.py:63
  186.6 5.5 %reshape.302 = f32[4,1,49152]{2,1,0:T(1,128)} reshape(f32[128,2,3,16,16]{4,3,2,1,0:T(8,128)} %bitcast.185) | data formatting | bytes 1572864
  192.1 4.2 all-to-all-start.3
  198.0 2.8 fusion.356
  200.8 6.4 %all-to-all-done.3 = f32[4,1,49152]{2,1,0:T(1,128)} async-done(((f32[4,1,49152]{2,1,0:T(1,128)}), f32[4,1,49152]{2,1,0:T(1,128)}, u32[]{:S(2)}, u32[]{:S(2)}) %all-to-all-start.3) | async-done | bytes 786464 | tf_op jit(solution)/shard_map/all_to_all | solution.py:186
  207.2 3.9 reduce.3
  211.1 4.9 %reshape.303 = f32[128,2,3,16,16]{4,3,2,1,0:T(8,128)} reshape(f32[4,49152]{1,0:T(4,128)S(1)} %reduce.3) | data formatting | bytes 1572864
  215.9 6.7 %copy.301 = f32[2,3,16,16,4,32]{5,3,2,4,1,0:T(8,128)} copy(f32[2,3,16,16,4,32]{3,2,1,0,5,4:T(8,128)} %bitcast.186) | data formatting | bytes 1572864 | tf_op jit(solution)/shard_map/all_to_all | solution.py:186
  222.7 3.8 fusion.343
  226.5 2.9 copy.303
  229.3 2.0 copy.302
  241.4 3.7 collective-permute-start.3
  245.5 2.6 copy.342
  248.1 2.5 copy.344
  250.6 2.5 copy.346
  253.1 2.6 copy.347
  255.7 2.5 copy.349
  258.2 2.5 copy.351
  270.6 37.9 %pmax.7 = f32[]{:T(128)} all-reduce(f32[]{:T(128)} %get-tuple-element.5), channel_id=1, replica_groups=mesh['row'=4,'col'=8] {'row','col'}, use_global_device_ids=true, to_apply=%region_1.2 | all-reduce | flops 1 | bytes 8 | tf_op jit(solution)/shard_map/pmax | solution.py:190
  313.2 9.8 %copy.310 = f32[3,34,18,128,2]{1,4,3,2,0:T(2,128)} copy(f32[3,34,18,128,2]{3,1,2,0,4:T(8,128)} %pad_maximum_fusion.3) | data formatting | bytes 3760128 | tf_op jit(solution)/shard_map/stack | solution.py:100
  323.0 12.1 %fusion.3 = (f32[3,32,1,18,256]{1,4,3,0,2:T(8,128)}, f32[3,32,1,18,256]{1,4,3,0,2:T(8,128)}) fusion(f32[3,34,18,256]{1,3,2,0:T(8,128)} %bitcast.175), kind=kLoop, calls=%fused_computation.6 | loop fusion | flops 2211840 | bytes 8847360 | tf_op jit(solution)/shard_map/stack | solution.py:110
  335.1 12.6 %pad_maximum_fusion = f32[3,32,2,18,256]{1,4,3,0,2:T(8,128)} fusion(f32[3,32,1,18,256]{1,4,3,0,2:T(8,128)} %get-tuple-element.8, f32[3,32,1,18,256]{1,4,3,0,2:T(8,128)} %get-tuple-element.7), kind=kLoop, calls=%fused_computation | loop fusion | flops 884736 | bytes 7077888 | tf_op jit(solution)/shard_map/stack | solution.py:110
  347.7 11.0 %copy.311 = f32[3,32,2,18,256]{4,2,1,3,0:T(2,128)} copy(f32[3,32,2,18,256]{1,4,3,0,2:T(8,128)} %pad_maximum_fusion) | data formatting | bytes 7077888 | tf_op jit(solution)/shard_map/stack | solution.py:110
  358.7 5.8 %reshape.287 = f32[3,64,18,256]{3,1,2,0:T(8,128)} reshape(f32[3,32,2,18,256]{4,2,1,3,0:T(2,128)} %copy.311) | data formatting | bytes 7077888 | tf_op jit(solution)/shard_map/reshape | solution.py:110
  364.5 4.8 %fusion.7 = (f32[3,64,16,1,256]{4,1,2,0,3:T(8,128)S(1)}, f32[3,64,16,1,256]{4,1,2,0,3:T(8,128)S(1)}) fusion(f32[3,64,18,256]{3,1,2,0:T(8,128)} %reshape.287), kind=kLoop, calls=%fused_computation.18 | loop fusion | flops 3932160 | bytes 15728640 | tf_op jit(solution)/shard_map/stack | solution.py:110
  381.7 23.9 %fusion.21 = f32[1,64,32,256]{3,1,2,0:T(8,128)S(1)} fusion(f32[64,32,3]{2,0,1:T(8,128)S(1)} %copy-done.15, f32[64,32,253]{2,0,1:T(8,128)S(1)} %copy-done.9, f32[64,32,2]{2,0,1:T(8,128)S(1)} %copy-done.16, f32[64,32,254]{2,0,1:T(8,128)S(1)} %copy-done.10, f32[64,32,1]{2,0,1:T(8,128)S(1)} %copy-done.17, f32[64,32,255]{2,0,1:T(8,128)S(1)} %copy-done.11, ...), kind=kLoop, calls=%fused_computation.57 | loop fusion | flops 152567808 | bytes 31457280 | tf_op jit(solution)/shard_map/stack | solution.py:197
  405.7 3.5 collective-permute-start.4
  409.4 6.4 %collective-permute-done.4 = f32[2,3,32,256]{3,1,2,0:T(4,128)S(1)} collective-permute-done((f32[2,3,32,256]{3,1,2,0:T(4,128)S(1)}, f32[2,3,32,256]{3,1,2,0:T(4,128)S(1)}, u32[]{:S(2)}, u32[]{:S(2)}) %collective-permute-start.4) | collective-permute-done | bytes 196640 | tf_op jit(solution)/shard_map/ppermute | solution.py:22
  415.8 4.7 collective-permute-done.5
  422.1 20.3 %fusion.76 = f32[1,64,32,256]{3,1,2,0:T(8,128)S(1)} fusion(f32[1,64,32,256]{3,1,2,0:T(8,128)S(1)} %fusion.21, f32[2,67,32,256]{3,1,2,0:T(8,128)S(1)} %get-tuple-element.21, f32[2,67,32,256]{3,1,2,0:T(8,128)S(1)} %get-tuple-element.20, f32[1,64,32,256]{3,1,2,0:T(8,128)S(1)} %bitcast.178), kind=kLoop, calls=%fused_computation.112 | loop fusion | flops 146276352 | bytes 31457280 | tf_op jit(solution)/shard_map/add | solution.py:130
  442.6 3.5 collective-permute-start.7
  446.1 8.9 %collective-permute-done.6 = f32[2,64,3,256]{3,1,2,0:T(8,128)S(1)} collective-permute-done((f32[2,64,3,256]{3,1,2,0:T(8,128)S(1)}, f32[2,64,3,256]{3,1,2,0:T(8,128)S(1)}, u32[]{:S(2)}, u32[]{:S(2)}) %collective-permute-start.6) | collective-permute-done | bytes 393248 | tf_op jit(solution)/shard_map/ppermute | solution.py:20
  456.0 19.0 %fusion.131 = f32[64,32,256]{2,0,1:T(8,128)S(1)} fusion(f32[64,38,256]{2,0,1:T(8,128)S(1)} %get-tuple-element.17, f32[64,38,256]{2,0,1:T(8,128)S(1)} %get-tuple-element.16), kind=kLoop, calls=%fused_computation.167 | loop fusion | flops 146276352 | bytes 31457280 | tf_op jit(solution)/shard_map/add | solution.py:130
  475.0 2.5 copy.326
  (133 shorter events, 60.9 us)
Async XLA Ops:
  0.0 1.1 copy-start
  58.8 25.8 %all-to-all-start.1 = ((f32[8,1,24576]{2,1,0:T(1,128)}), f32[8,1,24576]{2,1,0:T(1,128)S(1)}, u32[]{:S(2)}, u32[]{:S(2)}) async-start(f32[8,1,24576]{2,1,0:T(1,128)} %reshape.298), calls=%async_computation.1 | async-start | bytes 1572864 | tf_op jit(solution)/shard_map/all_to_all | solution.py:157
  123.4 10.1 %copy-start.2 = (f32[64,32,256]{2,1,0:T(8,128)S(1)}, f32[64,32,256]{2,1,0:T(8,128)}, u32[]{:S(2)}) copy-start(f32[64,32,256]{2,1,0:T(8,128)} %param.3) | copy-start | bytes 6291460
  129.0 25.4 %all-to-all-start.2 = ((f32[8,1,24576]{2,1,0:T(1,128)}), f32[8,1,24576]{2,1,0:T(1,128)}, u32[]{:S(2)}, u32[]{:S(2)}) async-start(f32[8,1,24576]{2,1,0:T(1,128)} %reshape.300), calls=%async_computation.2 | async-start | bytes 1572864 | tf_op jit(solution)/shard_map/all_to_all | solution.py:180
  192.1 15.1 %all-to-all-start.3 = ((f32[4,1,49152]{2,1,0:T(1,128)}), f32[4,1,49152]{2,1,0:T(1,128)}, u32[]{:S(2)}, u32[]{:S(2)}) async-start(f32[4,1,49152]{2,1,0:T(1,128)} %reshape.302), calls=%async_computation.3 | async-start | bytes 1572864 | tf_op jit(solution)/shard_map/all_to_all | solution.py:186
  234.9 4.8 %collective-permute-start = (f32[3,1,16,128]{3,1,2,0:T(1,128)S(1)}, f32[3,1,16,128]{3,1,2,0:T(1,128)S(1)}, u32[]{:S(2)}, u32[]{:S(2)}) collective-permute-start(f32[3,1,16,128]{3,1,2,0:T(1,128)S(1)} %get-tuple-element.64), channel_id=1, source_target_pairs={{0,8},{8,16},{16,24},{24,0},{1,9},{9,17},{17,25},{25,1},{2,10},{10... | collective-permute-start | bytes 73736 | tf_op jit(solution)/shard_map/ppermute | solution.py:20
  236.4 3.8 collective-permute-start.1
  241.3 67.8 %collective-permute-start.2 = (f32[3,34,1,128]{3,1,0,2:T(8,128)S(1)}, f32[3,34,1,128]{3,1,0,2:T(8,128)S(1)}, u32[]{:S(2)}, u32[]{:S(2)}) collective-permute-start(f32[3,34,1,128]{3,1,0,2:T(8,128)S(1)} %get-tuple-element.60), channel_id=1, source_target_pairs={{0,1},{1,2},{2,3},{3,4},{4,5},{5,6},{6,7},{7,0},{8,9},{9,10},{10,1... | collective-permute-start | bytes 156680 | tf_op jit(solution)/shard_map/ppermute | solution.py:20
  241.4 4.1 copy-start.5
  241.4 67.8 %collective-permute-start.3 = (f32[3,34,1,128]{3,1,0,2:T(8,128)S(1)}, f32[3,34,1,128]{3,1,0,2:T(8,128)S(1)}, u32[]{:S(2)}, u32[]{:S(2)}) collective-permute-start(f32[3,34,1,128]{3,1,0,2:T(8,128)S(1)} %get-tuple-element.61), channel_id=1, source_target_pairs={{1,0},{2,1},{3,2},{4,3},{5,4},{6,5},{7,6},{0,7},{9,8},{10,9},{11,1... | collective-permute-start | bytes 156680 | tf_op jit(solution)/shard_map/ppermute | solution.py:22
  245.5 2.6 copy-start.6
  248.1 2.5 copy-start.8
  250.6 2.5 copy-start.7
  253.1 2.6 copy-start.4
  255.7 2.5 copy-start.3
  258.2 2.5 copy-start.22
  265.6 3.2 copy-start.21
  309.7 1.2 copy-start.23
  372.7 6.2 %copy-start.19 = (f32[64,32,2]{2,0,1:T(8,128)S(1)}, f32[64,32,2]{2,0,1:T(8,128)}, u32[]{:S(2)}) copy-start(f32[64,32,2]{2,0,1:T(8,128)} %copy.350) | copy-start | bytes 49156
  372.7 6.2 %copy-start.20 = (f32[64,32,3]{2,0,1:T(8,128)S(1)}, f32[64,32,3]{2,0,1:T(8,128)}, u32[]{:S(2)}) copy-start(f32[64,32,3]{2,0,1:T(8,128)} %copy.352) | copy-start | bytes 73732
  373.4 5.5 %copy-start.15 = (f32[64,32,3]{2,0,1:T(8,128)S(1)}, f32[64,32,3]{2,0,1:T(8,128)}, u32[]{:S(2)}) copy-start(f32[64,32,3]{2,0,1:T(8,128)} %copy.341) | copy-start | bytes 73732
  373.4 5.5 %copy-start.16 = (f32[64,32,2]{2,0,1:T(8,128)S(1)}, f32[64,32,2]{2,0,1:T(8,128)}, u32[]{:S(2)}) copy-start(f32[64,32,2]{2,0,1:T(8,128)} %copy.343) | copy-start | bytes 49156
  373.5 5.5 %copy-start.17 = (f32[64,32,1]{2,0,1:T(8,128)S(1)}, f32[64,32,1]{2,0,1:T(8,128)}, u32[]{:S(2)}) copy-start(f32[64,32,1]{2,0,1:T(8,128)} %copy.345) | copy-start | bytes 24580
  373.5 5.5 %copy-start.18 = (f32[64,32,1]{2,0,1:T(8,128)S(1)}, f32[64,32,1]{2,0,1:T(8,128)}, u32[]{:S(2)}) copy-start(f32[64,32,1]{2,0,1:T(8,128)} %copy.348) | copy-start | bytes 24580
  375.2 3.7 copy-start.13
  375.2 3.8 copy-start.14
  376.9 3.0 copy-start.11
  376.9 3.6 copy-start.12
  378.6 2.4 copy-start.9
  378.6 3.0 copy-start.10
  405.7 10.2 %collective-permute-start.4 = (f32[2,3,32,256]{3,1,2,0:T(4,128)S(1)}, f32[2,3,32,256]{3,1,2,0:T(4,128)S(1)}, u32[]{:S(2)}, u32[]{:S(2)}) collective-permute-start(f32[2,3,32,256]{3,1,2,0:T(4,128)S(1)} %get-tuple-element.22), channel_id=1, source_target_pairs={{8,0},{16,8},{24,16},{0,24},{9,1},{17,9},{25,17},{1,25},{10,2},{18... | collective-permute-start | bytes 589832 | tf_op jit(solution)/shard_map/ppermute | solution.py:22
  409.2 11.4 %collective-permute-start.5 = (f32[2,3,32,256]{3,1,2,0:T(4,128)S(1)}, f32[2,3,32,256]{3,1,2,0:T(4,128)S(1)}, u32[]{:S(2)}, u32[]{:S(2)}) collective-permute-start(f32[2,3,32,256]{3,1,2,0:T(4,128)S(1)} %get-tuple-element.23), channel_id=1, source_target_pairs={{0,8},{8,16},{16,24},{24,0},{1,9},{9,17},{17,25},{25,1},{2,10},{10... | collective-permute-start | bytes 589832 | tf_op jit(solution)/shard_map/ppermute | solution.py:20
  442.5 12.5 %collective-permute-start.6 = (f32[2,64,3,256]{3,1,2,0:T(8,128)S(1)}, f32[2,64,3,256]{3,1,2,0:T(8,128)S(1)}, u32[]{:S(2)}, u32[]{:S(2)}) collective-permute-start(f32[2,64,3,256]{3,1,2,0:T(8,128)S(1)} %get-tuple-element.18), channel_id=1, source_target_pairs={{0,1},{1,2},{2,3},{3,4},{4,5},{5,6},{6,7},{7,0},{8,9},{9,10},{10,1... | collective-permute-start | bytes 1179656 | tf_op jit(solution)/shard_map/ppermute | solution.py:20
  442.6 12.4 %collective-permute-start.7 = (f32[2,64,3,256]{3,1,2,0:T(8,128)S(1)}, f32[2,64,3,256]{3,1,2,0:T(8,128)S(1)}, u32[]{:S(2)}, u32[]{:S(2)}) collective-permute-start(f32[2,64,3,256]{3,1,2,0:T(8,128)S(1)} %get-tuple-element.19), channel_id=1, source_target_pairs={{1,0},{2,1},{3,2},{4,3},{5,4},{6,5},{7,6},{0,7},{9,8},{10,9},{11,1... | collective-permute-start | bytes 1179656 | tf_op jit(solution)/shard_map/ppermute | solution.py:22
  456.0 21.6 %copy-start.1 = (f32[3,32,16,128]{3,2,1,0:T(8,128)S(1)}, f32[3,32,16,128]{3,2,1,0:T(8,128)}, u32[]{:S(2)}) copy-start(f32[3,32,16,128]{3,2,1,0:T(8,128)} %param.2) | copy-start | bytes 2359300
where the time goes:
time: 483 us; the launch traced here: 478 us
  local copies, waits for them, and re-layouts  199 us (41%)
  other arithmetic  115 us (24%)
  waiting for transfers between devices  64.2 us (13%)
  blocking collectives  54.5 us (11%)
  starting transfers between devices  27.3 us (6%)
  matrix products  16 us (3%)
    unnamed x69, local copies, waits for them, and re-layouts  66.4 us
    add x2, other arithmetic, remesh_rim(): summed = summed + values * kernel_weight(offset - moved)  39.3 us
    pmax x1, blocking collectives, shards(): velocity_peak = lax.pmax(jnp.max(jnp.abs(velocity)), ('row', 'col'))  37.9 us
    another operation x3, other arithmetic, refine_rim(): jnp.stack([lower, upper], axis=grid_axis + 1)  29.5 us
    another operation x1, other arithmetic, shards(): rows_input = jnp.stack([swept, displaced[1]])  23.9 us
    all_to_all x1, waiting for transfers between devices, shards(): lax.all_to_all(spectrum, 'col', split_axis=4, concat_axis=2, tiled=True)  20.6 us
    another operation x3, local copies, waits for them, and re-layouts, rotate(): jnp.stack([real_cos - direction * imag_sin, imag_cos + direction * real_s...  18.6 us
    all_to_all x1, blocking collectives, shards(): lax.all_to_all(forward, 'row', split_axis=4, concat_axis=2, tiled=True)  16.6 us
  transfers between devices with their start and end apart: 11, of which 8 were waited for; matrix products, arithmetic and copies ran while one was open for 8% of the time, Pallas kernels for 0%

commit v1 on v0

v1 whole, which is shorter than its diff:
```python
import functools

import jax
import jax.numpy as jnp
import numpy as np
from jax import lax
from jax.experimental import pallas as pl
from jax.experimental.pallas import tpu as pltpu
from jax.sharding import PartitionSpec as P

COURANT = 0.9
EPSILON = 1e-06
HIGHEST = lax.Precision.HIGHEST
MESH = pl.DeviceIdType.MESH


def refine_matrix(n):
    matrix = np.zeros((2 * n, n))
    for j in range(n):
        matrix[2 * j, j] += 0.75
        matrix[2 * j, (j - 1) % n] += 0.25
        matrix[2 * j + 1, j] += 0.75
        matrix[2 * j + 1, (j + 1) % n] += 0.25
    return matrix


def tables(n, rows, padded):
    index = np.arange(n)
    angle = 2.0 * np.pi * (index[:, None] * index[None, :] % n) / n
    cos, sin = np.cos(angle), np.sin(angle)
    half = n // 2
    forward_x = np.concatenate([cos[:, :half], -sin[:, :half]], axis=1)
    weight = np.where(index[:half] == 0, 1.0, 2.0)[:, None]
    back = np.concatenate([cos[:half] * weight, -sin[:half] * weight], axis=0)
    back_x = np.concatenate([back @ refine_matrix(n).T, back], axis=1)
    both = np.concatenate([cos, sin], axis=0)
    count = n // rows
    picked = np.zeros((2, rows, padded, n))
    for r in range(rows):
        lines = [r * count + i for i in range(count)] + [(r * count - 1) % n, (r * count + count) % n]
        picked[0, r, : count + 2] = cos[lines]
        picked[1, r, : count + 2] = sin[lines]
    inverse_y = picked.reshape(2 * rows * padded, n)
    return [t.astype(np.float32) for t in (forward_x, both, inverse_y, back_x)]


def dot(a, b):
    return jnp.dot(a, b, precision=HIGHEST, preferred_element_type=jnp.float32)


def spread(field, displace):
    a = jnp.abs(displace)
    b = 1.0 - a
    q = field * (a * b) * (1.0 / 24.0)
    p3 = q * (a * a) * (7.0 - 5.0 * a)
    m2 = q * (b * b) * (7.0 - 5.0 * b)
    p2 = q * (((25.0 * a - 36.0) * a - 3.0) * a - 2.0 - 0.0)
    m1 = q * (((25.0 * b - 36.0) * b - 3.0) * b - 2.0 - 0.0)
    p1 = field * a - 2.0 * p2 - 3.0 * p3 + m1 + 2.0 * m2
    c0 = field - p1 - p2 - p3 - m1 - m2
    up = displace >= 0.0
    zero = jnp.zeros_like(p3)
    return {
        0: c0,
        1: jnp.where(up, p1, m1),
        -1: jnp.where(up, m1, p1),
        2: jnp.where(up, p2, m2),
        -2: jnp.where(up, m2, p2),
        3: jnp.where(up, p3, zero),
        -3: jnp.where(up, zero, p3),
    }


def body(
    rows, cols, jrows,
    vort, scalar, fx, both, iy, bx, out,
    tmp, g1, r1, s2, r2, s3, r3, w4, r4, fine, peaks, pack, disp_z, acc, halo_y, zr, zl, zin_r, zin_l,
    sem1, sem2, sem3, sem4, sem4h, semp, semy, semz,
):
    n = vort.shape[2]
    ny, nz = n // rows, n // cols
    zc = nz // rows
    devices = rows * cols
    kc = n // devices
    chunk = zc * jrows
    padded = ny + 8
    zp = fine.shape[1] // (ny + 2)
    nf, nzf = 2 * ny, 2 * nz
    half = n // 2
    row, col = lax.axis_index("row"), lax.axis_index("col")
    me = col * rows + row

    def where_is(index):
        return (lax.rem(index, rows), index // rows)

    barrier = pltpu.get_barrier_semaphore()

    def greet(p, carry):
        pl.semaphore_signal(barrier, inc=1, device_id=where_is(lax.rem(me + p, devices)), device_id_type=MESH)
        return carry

    lax.fori_loop(1, devices, greet, 0)

    lane = lax.broadcasted_iota(jnp.int32, (1, n), 1)
    sign = jnp.where(lane < half, 1.0, -1.0)

    def turn(product, direction):
        count = product.shape[0] // 2
        swapped = pltpu.roll(product[count:], half, axis=1)
        return product[:count] + swapped * (sign * direction)

    for c in range(3):
        tmp[c] = dot(vort[c], fx[...])
    for z in range(nz):
        for c in range(3):
            g1[z // zc, pl.ds(((z % zc) * 3 + c) * ny, ny), :] = tmp[c, pl.ds(z, ny, stride=nz), :]
    pl.semaphore_wait(barrier, devices - 1)

    def copy_row(source, target, sems, p):
        peer = lax.rem(row + p, rows)
        return pltpu.make_async_remote_copy(
            src_ref=source.at[peer], dst_ref=target.at[row], send_sem=sems.at[0, p], recv_sem=sems.at[1, p],
            device_id=(peer, col), device_id_type=MESH)

    first = [copy_row(g1, r1, sem1, p) for p in range(1, rows)]
    for copy in first:
        copy.start()
    r1[row] = g1[row]
    for copy in first:
        copy.wait()

    for z in range(zc):
        for c in range(3):
            lines = jnp.concatenate([r1[r, pl.ds((z * 3 + c) * ny, ny), :] for r in range(rows)], axis=0)
            modes = turn(dot(both[...], lines), 1.0)
            for k in range(kc):
                s2[pl.ds(z * jrows + k * 3 + c, devices, stride=chunk), :] = modes[k * devices:(k + 1) * devices]

    def exchange(source, target, sems):
        def make(p):
            peer = lax.rem(me + p, devices)
            return pltpu.make_async_remote_copy(
                src_ref=source.at[pl.ds(pl.multiple_of(peer * chunk, 8), chunk)],
                dst_ref=target.at[pl.ds(pl.multiple_of(me * chunk, 8), chunk)],
                send_sem=sems.at[0, p], recv_sem=sems.at[1, p],
                device_id=where_is(peer), device_id_type=MESH)

        def start(p, carry):
            make(p).start()
            return carry

        def wait(p, carry):
            make(p).wait()
            return carry

        lax.fori_loop(1, devices, start, 0)
        own = pl.ds(pl.multiple_of(me * chunk, 8), chunk)
        target[own, :] = source[own, :]
        lax.fori_loop(1, devices, wait, 0)

    exchange(s2, r2, sem2)

    xi = lax.broadcasted_iota(jnp.int32, (n, n), 1)
    zi = lax.broadcasted_iota(jnp.int32, (n, n), 0)
    kx = jnp.where(xi < half, xi, xi - half).astype(jnp.float32)
    kz = jnp.where(zi < half, zi, zi - n).astype(jnp.float32)
    for k in range(kc):
        yi = k * devices + me
        ky_int = yi - jnp.where(yi < half, 0, n)
        ky = jnp.full((n, n), ky_int, jnp.int32).astype(jnp.float32)
        square = kx * kx + ky * ky + kz * kz
        keep = (square > 0.0) & (zi != half) & (jnp.full((n, n), yi, jnp.int32) != half)
        factor = jnp.where(keep, 1.0 / jnp.maximum(square, 1.0), 0.0) * (1.0 / (n * n * n))
        ox, oy, oz = [turn(dot(both[...], r2[pl.ds(k * 3 + c, n, stride=jrows), :]), 1.0) for c in range(3)]
        for c, cross in enumerate((ky * oz - kz * oy, kz * ox - kx * oz, kx * oy - ky * ox)):
            hat = pltpu.roll(cross * factor, half, axis=1) * (-sign)
            s3[pl.ds(k * 3 + c, n, stride=jrows), :] = turn(dot(both[...], hat), -1.0)

    exchange(s3, r3, sem3)

    for z in range(zc):
        for c in range(3):
            modes = jnp.concatenate(
                [r3[pl.ds(z * jrows + k * 3 + c, devices, stride=chunk), :] for k in range(kc)], axis=0)
            lines = turn(dot(iy[...], modes), -1.0)
            for r in range(rows):
                w4[r, z, pl.ds(c * padded, padded), :] = lines[r * padded:(r + 1) * padded]

    def copy_back(p):
        peer = lax.rem(row + p, rows)
        return pltpu.make_async_remote_copy(
            src_ref=w4.at[peer], dst_ref=r4.at[pl.ds(1 + row * zc, zc)], send_sem=sem4.at[0, p],
            recv_sem=sem4.at[1, p], device_id=(peer, col), device_id_type=MESH)

    def copy_layer(r, top):
        step = 1 if top else cols - 1
        return pltpu.make_async_remote_copy(
            src_ref=w4.at[r, zc - 1 if top else 0], dst_ref=r4.at[0 if top else nz + 1],
            send_sem=sem4h.at[0 if top else 1, r], recv_sem=sem4h.at[0 if top else 1, rows],
            device_id=(r, lax.rem(col + step, cols)), device_id_type=MESH)

    @pl.when(row == rows - 1)
    def _():
        for r in range(rows):
            copy_layer(r, True).start()

    @pl.when(row == 0)
    def _():
        for r in range(rows):
            copy_layer(r, False).start()

    last = [copy_back(p) for p in range(1, rows)]
    for copy in last:
        copy.start()
    r4[pl.ds(1 + row * zc, zc)] = w4[row]
    for copy in last:
        copy.wait()
    copy_layer(0, True).wait_recv()
    copy_layer(0, False).wait_recv()

    @pl.when(row == rows - 1)
    def _():
        for r in range(rows):
            copy_layer(r, True).wait_send()

    @pl.when(row == 0)
    def _():
        for r in range(rows):
            copy_layer(r, False).wait_send()

    top = jnp.zeros((8, n), jnp.float32)
    for z in range(nz + 2):
        product = dot(r4[z], bx[...])
        size = jnp.abs(product[:, 2 * n:])
        top = jnp.maximum(top, jnp.max(size.reshape(size.shape[0] // 8, 8, n), axis=0))
        for c in range(3):
            for h in range(2):
                part = product[c * padded:(c + 1) * padded, h * n:(h + 1) * n]
                fine[c * 2 + h, pl.ds(zp + z, ny, stride=zp), :] = part[:ny]
                fine[c * 2 + h, pl.ds(z, 1), :] = part[ny:ny + 1]
                fine[c * 2 + h, pl.ds((ny + 1) * zp + z, 1), :] = part[ny + 1:ny + 2]
    peaks[me] = top

    def send_peak(p):
        return pltpu.make_async_remote_copy(
            src_ref=peaks.at[me], dst_ref=peaks.at[me], send_sem=semp.at[0, p], recv_sem=semp.at[1, p],
            device_id=where_is(lax.rem(me + p, devices)), device_id_type=MESH)

    def peak_start(p, carry):
        send_peak(p).start()
        return carry

    def peak_wait(p, carry):
        send_peak(p).wait()
        return carry

    lax.fori_loop(1, devices, peak_start, 0)

    def clear(y, carry):
        acc[y] = jnp.zeros((nzf, 2 * n), jnp.float32)
        return carry

    lax.fori_loop(0, nf + 6, clear, 0)
    lax.fori_loop(1, devices, peak_wait, 0)
    scale = COURANT / (jnp.max(peaks[...]) + EPSILON)

    def sweep(j):
        def plane(ch, y):
            return fine[ch, pl.ds(pl.multiple_of(y * zp, 8), zp), :]

        for c in range(3):
            for h in range(2):
                middle = plane(c * 2 + h, j + 1) * (0.75 * scale)
                for side in range(2):
                    line = middle + plane(c * 2 + h, j + 2 * side) * (0.25 * scale)
                    inner = 0.75 * line[1:nz + 1]
                    pack[side * 6 + c * 2 + h, pl.ds(0, nz, stride=2), :] = inner + 0.25 * line[0:nz]
                    pack[side * 6 + c * 2 + h, pl.ds(1, nz, stride=2), :] = inner + 0.25 * line[2:nz + 2]
        for side in range(2):
            y = 2 * j + side
            dx, dy, dz = [
                jnp.concatenate([pack[side * 6 + c * 2], pack[side * 6 + c * 2 + 1]], axis=1) for c in range(3)]
            disp_z[y] = dz
            parts = spread(scalar[y], dx)
            swept = parts[0]
            for offset in (1, 2, 3):
                swept = swept + pltpu.roll(parts[offset], offset, axis=1)
                swept = swept + pltpu.roll(parts[-offset], 2 * n - offset, axis=1)
            parts = spread(swept, dy)
            for offset in range(-3, 4):
                acc[y + 3 + offset] += parts[offset]

    def edge(i):
        return jnp.where(i < 2, i, ny - 4 + i)

    def sweep_edge(i, carry):
        sweep(edge(i))
        return carry

    def sweep_inner(j, carry):
        sweep(j)
        return carry

    lax.fori_loop(0, 4, sweep_edge, 0)

    def copy_y(up):
        step = 1 if up else rows - 1
        side = 0 if up else 1
        return pltpu.make_async_remote_copy(
            src_ref=acc.at[pl.ds(nf + 3 if up else 0, 3)], dst_ref=halo_y.at[side], send_sem=semy.at[0, side],
            recv_sem=semy.at[1, side], device_id=(lax.rem(row + step, rows), col), device_id_type=MESH)

    copy_y(True).start()
    copy_y(False).start()
    lax.fori_loop(2, ny - 2, sweep_inner, 0)

    row_of = lax.broadcasted_iota(jnp.int32, (nzf, 2 * n), 0)
    row8 = lax.broadcasted_iota(jnp.int32, (8, 2 * n), 0)

    def lift(p):
        tiles = []
        for side in range(2):
            y = 2 * p + side
            parts = spread(acc[y + 3], disp_z[y])
            kept = parts[0]
            above = jnp.zeros((8, 2 * n), jnp.float32)
            below = jnp.zeros((8, 2 * n), jnp.float32)
            for offset in (1, 2, 3):
                moved = pltpu.roll(parts[offset], offset, axis=0)
                kept = kept + jnp.where(row_of >= offset, moved, 0.0)
                above = above + jnp.where(row8 < offset, moved[:8], 0.0)
                moved = pltpu.roll(parts[-offset], nzf - offset, axis=0)
                kept = kept + jnp.where(row_of < nzf - offset, moved, 0.0)
                below = below + jnp.where(row8 >= 8 - offset, moved[nzf - 8:], 0.0)
            out[y] = kept
            tiles.append((above, below))
        zr[p] = tiles[0][0] + pltpu.roll(tiles[1][0], 4, axis=0)
        zl[p] = tiles[0][1] + pltpu.roll(tiles[1][1], 4, axis=0)

    def lift_inner(p, carry):
        lift(p)
        return carry

    def lift_edge(i, carry):
        lift(edge(i))
        return carry

    def copy_z(index):
        start, count = ((2, ny - 4), (0, 2), (ny - 2, 2))[index]
        here = pl.ds(start, count)
        return [
            pltpu.make_async_remote_copy(
                src_ref=source.at[here], dst_ref=target.at[here], send_sem=semz.at[0, side, index],
                recv_sem=semz.at[1, side, index], device_id=(row, lax.rem(col + step, cols)), device_id_type=MESH)
            for side, source, target, step in ((0, zr, zin_r, 1), (1, zl, zin_l, cols - 1))]

    lax.fori_loop(2, ny - 2, lift_inner, 0)
    for copy in copy_z(0):
        copy.start()
    copy_y(True).wait()
    copy_y(False).wait()
    for i in range(3):
        acc[3 + i] += halo_y[0, i]
        acc[nf + i] += halo_y[1, i]
    lax.fori_loop(0, 4, lift_edge, 0)
    for index in (1, 2):
        for copy in copy_z(index):
            copy.start()

    def finish(p, carry):
        low, high = zin_r[p], zin_l[p]
        for side in range(2):
            if side:
                low, high = pltpu.roll(low, 4, axis=0), pltpu.roll(high, 4, axis=0)
            out[2 * p + side, :8, :] += jnp.where(row8 < 3, low, 0.0)
            out[2 * p + side, nzf - 8:, :] += jnp.where(row8 >= 5, high, 0.0)
        return carry

    for index, (start, stop) in enumerate(((2, ny - 2), (0, 2), (ny - 2, ny))):
        for copy in copy_z(index):
            copy.wait()
        lax.fori_loop(start, stop, finish, 0)


def shards(rows, cols, vorticity, scalar):
    n = vorticity.shape[3]
    ny, nz = vorticity.shape[1], vorticity.shape[2]
    devices = rows * cols
    zc, kc = nz // rows, n // devices
    jrows = kc * 3
    while zc * jrows % 8:
        jrows += 1
    padded = ny + 8
    zp = (nz + 2 + 7) // 8 * 8
    nf, nzf = 2 * ny, 2 * nz
    f32 = jnp.float32
    total = devices * zc * jrows
    vmem = pl.BlockSpec(memory_space=pltpu.VMEM)
    dma = pltpu.SemaphoreType.DMA
    return pl.pallas_call(
        functools.partial(body, rows, cols, jrows),
        out_shape=jax.ShapeDtypeStruct((nf, nzf, 2 * n), f32),
        in_specs=[vmem] * 6,
        out_specs=vmem,
        scratch_shapes=[
            pltpu.VMEM((3, ny * nz, n), f32),
            pltpu.VMEM((rows, zc * 3 * ny, n), f32),
            pltpu.VMEM((rows, zc * 3 * ny, n), f32),
            pltpu.VMEM((total, n), f32),
            pltpu.VMEM((total, n), f32),
            pltpu.VMEM((total, n), f32),
            pltpu.VMEM((total, n), f32),
            pltpu.VMEM((rows, zc, 3 * padded, n), f32),
            pltpu.VMEM((nz + 2, 3 * padded, n), f32),
            pltpu.VMEM((6, (ny + 2) * zp, n), f32),
            pltpu.VMEM((devices, 8, n), f32),
            pltpu.VMEM((12, nzf, n), f32),
            pltpu.VMEM((nf, nzf, 2 * n), f32),
            pltpu.VMEM((nf + 6, nzf, 2 * n), f32),
            pltpu.VMEM((2, 3, nzf, 2 * n), f32),
            pltpu.VMEM((ny, 8, 2 * n), f32),
            pltpu.VMEM((ny, 8, 2 * n), f32),
            pltpu.VMEM((ny, 8, 2 * n), f32),
            pltpu.VMEM((ny, 8, 2 * n), f32),
            dma((2, rows)),
            dma((2, devices)),
            dma((2, devices)),
            dma((2, rows)),
            dma((2, rows + 1)),
            dma((2, devices)),
            dma((2, 2)),
            dma((2, 2, 3)),
        ],
        compiler_params=pltpu.CompilerParams(
            collective_id=0, has_side_effects=True, vmem_limit_bytes=56 * 1024 * 1024),
    )(vorticity.reshape(3, ny * nz, n), scalar, *[jnp.asarray(t) for t in tables(n, rows, padded)])


def solution(mesh):
    rows, cols = mesh.shape["row"], mesh.shape["col"]
    return jax.shard_map(
        functools.partial(shards, rows, cols),
        mesh=mesh,
        in_specs=(P(None, "row", "col", None), P("row", "col", None)),
        out_specs=P("row", "col", None),
        check_vma=False,
    )
```

time: 483 us -> 117 us (0.24); the launches traced: 478 us -> 117 us
  local copies, waits for them, and re-layouts: 199 us -> 3.16 us
  other arithmetic: 115 us -> 0 us
  Pallas kernels: 0 us -> 114 us
  waiting for transfers between devices: 64.2 us -> 0 us
  blocking collectives: 54.5 us -> 0 us
  starting transfers between devices: 27.3 us -> 0 us
  matrix products: 16 us -> 0 us
    pallas_call x0 -> x1, Pallas kernels: none -> 114 us  [shards(): pl.pallas_call(functools.partial(body, rows, cols, jrows), out_shape=jax....]
    unnamed x69 -> x1, local copies, waits for them, and re-layouts: 66.4 us -> 3.16 us
    another operation x9 -> x0, other arithmetic: 55.4 us -> none  [the longest x3 29.5 us: refine_rim(): jnp.stack([lower, upper], axis=grid_axis + 1)]
    all_to_all x3 -> x0, waiting for transfers between devices: 42.2 us -> none  [the longest x1 20.6 us: shards(): lax.all_to_all(spectrum, 'col', split_axis=4, concat_axis=2, tiled=True)]
    another operation x6 -> x0, local copies, waits for them, and re-layouts: 41.8 us -> none  [the longest x3 18.6 us: rotate(): jnp.stack([real_cos - direction * imag_sin, imag_cos + direction * real_s...]
    add x4 -> x0, other arithmetic: 40.1 us -> none  [the longest x2 39.3 us: remesh_rim(): summed = summed + values * kernel_weight(offset - moved)]
    pmax x1 -> x0, blocking collectives: 37.9 us -> none  [shards(): velocity_peak = lax.pmax(jnp.max(jnp.abs(velocity)), ('row', 'col'))]
    slice x23 -> x0, local copies, waits for them, and re-layouts: 37.1 us -> none  [the longest x6 11 us: remesh_roll(): jnp.roll(field, offset, grid_axis)]
  transfers between devices with their start and end apart: 11 -> 0, of which waited for: 8 -> 0; matrix products, arithmetic and copies ran while one was open for 8% -> 0% of each run, Pallas kernels for 0% -> 0%
where the time goes in v1:
time: 117 us
  Pallas kernels  114 us (97%)
  local copies, waits for them, and re-layouts  3.16 us (3%)
    pallas_call x1, Pallas kernels, shards(): pl.pallas_call(functools.partial(body, rows, cols, jrows), out_shape=jax....  114 us
    unnamed x1, local copies, waits for them, and re-layouts  3.16 us

profile of v1, /device:TPU:0, one launch (start us, length us, event | category | flops | bytes accessed | tf_op | source)
XLA Modules:
  0.0 116.7 jit_solution(13363698980321452870)
XLA Ops:
  0.0 113.5 %shard_map.64 = f32[64,32,256]{2,1,0:T(8,128)} custom-call(f32[3,512,128]{2,1,0:T(8,128)} %bitcast.1, f32[64,32,256]{2,1,0:T(8,128)} %scalar.1, f32[128,128]{1,0:T(8,128)} %constant.8.clone.fx, f32[256,128]{1,0:T(8,128)} %constant.9.clone.both, f32[320,128]{1,0:T(8,128)} %constant.10.clone.iy, f32[128,384]{1,0:T(8,128)} %constant.11.clone.bx), custom_call_target="tpu_custom_call" | custom-call | tf_op jit(solution)/shard_map/pallas_call | solution.py:400
  113.5 3.2 %copy.8 = f32[64,32,256]{2,1,0:T(8,128)} copy(f32[64,32,256]{2,1,0:T(8,128)} %shard_map.64) | data formatting | bytes 4194304

commit v2 on v1

--- a/solution.py
+++ b/solution.py
@@ -10,7 +10,7 @@
 
 COURANT = 0.9
 EPSILON = 1e-06
-HIGHEST = lax.Precision.HIGHEST
+HIGH = lax.Precision.HIGH
 MESH = pl.DeviceIdType.MESH
 
 
@@ -45,7 +45,7 @@
 
 
 def dot(a, b):
-    return jnp.dot(a, b, precision=HIGHEST, preferred_element_type=jnp.float32)
+    return jnp.dot(a, b, precision=HIGH, preferred_element_type=jnp.float32)
 
 
 def spread(field, displace):
@@ -74,7 +74,7 @@
 def body(
     rows, cols, jrows,
     vort, scalar, fx, both, iy, bx, out,
-    tmp, g1, r1, s2, r2, s3, r3, w4, r4, fine, peaks, pack, disp_z, acc, halo_y, zr, zl, zin_r, zin_l,
+    tmp, g1, r1, s2, r2, omega, factor, s3, r3, w4, r4, fine, peaks, pack, disp_z, acc, halo_y, zr, zl, zin_r, zin_l,
     sem1, sem2, sem3, sem4, sem4h, semp, semy, semz,
 ):
     n = vort.shape[2]
@@ -109,136 +109,148 @@
         swapped = pltpu.roll(product[count:], half, axis=1)
         return product[:count] + swapped * (sign * direction)
 
+    def copy_row(c, p):
+        peer = lax.rem(row + p, rows)
+        return pltpu.make_async_remote_copy(
+            src_ref=g1.at[c, peer], dst_ref=r1.at[c, row], send_sem=sem1.at[0, c, p], recv_sem=sem1.at[1, c, p],
+            device_id=(peer, col), device_id_type=MESH)
+
     for c in range(3):
         tmp[c] = dot(vort[c], fx[...])
-    for z in range(nz):
-        for c in range(3):
-            g1[z // zc, pl.ds(((z % zc) * 3 + c) * ny, ny), :] = tmp[c, pl.ds(z, ny, stride=nz), :]
-    pl.semaphore_wait(barrier, devices - 1)
-
-    def copy_row(source, target, sems, p):
-        peer = lax.rem(row + p, rows)
-        return pltpu.make_async_remote_copy(
-            src_ref=source.at[peer], dst_ref=target.at[row], send_sem=sems.at[0, p], recv_sem=sems.at[1, p],
-            device_id=(peer, col), device_id_type=MESH)
-
-    first = [copy_row(g1, r1, sem1, p) for p in range(1, rows)]
-    for copy in first:
-        copy.start()
-    r1[row] = g1[row]
-    for copy in first:
-        copy.wait()
-
-    for z in range(zc):
-        for c in range(3):
-            lines = jnp.concatenate([r1[r, pl.ds((z * 3 + c) * ny, ny), :] for r in range(rows)], axis=0)
+        for z in range(nz):
+            g1[c, z // zc, pl.ds((z % zc) * ny, ny), :] = tmp[c, pl.ds(z, ny, stride=nz), :]
+        if c == 0:
+            pl.semaphore_wait(barrier, devices - 1)
+        for p in range(1, rows):
+            copy_row(c, p).start()
+        r1[c, row] = g1[c, row]
+
+    def make(source, target, sems, c, p):
+        peer = lax.rem(me + p, devices)
+        return pltpu.make_async_remote_copy(
+            src_ref=source.at[c, pl.ds(pl.multiple_of(peer * chunk, 8), chunk)],
+            dst_ref=target.at[c, pl.ds(pl.multiple_of(me * chunk, 8), chunk)],
+            send_sem=sems.at[0, c, p], recv_sem=sems.at[1, c, p],
+            device_id=where_is(peer), device_id_type=MESH)
+
+    def send(source, target, sems, c):
+        def start(p, carry):
+            make(source, target, sems, c, p).start()
+            return carry
+
+        lax.fori_loop(1, devices, start, 0)
+        own = pl.ds(pl.multiple_of(me * chunk, 8), chunk)
+        target[c, own, :] = source[c, own, :]
+
+    def receive(source, target, sems, c):
+        def wait(p, carry):
+            make(source, target, sems, c, p).wait()
+            return carry
+
+        lax.fori_loop(1, devices, wait, 0)
+
+    for c in range(3):
+        for p in range(1, rows):
+            copy_row(c, p).wait()
+        for z in range(zc):
+            lines = jnp.concatenate([r1[c, r, pl.ds(z * ny, ny), :] for r in range(rows)], axis=0)
             modes = turn(dot(both[...], lines), 1.0)
             for k in range(kc):
-                s2[pl.ds(z * jrows + k * 3 + c, devices, stride=chunk), :] = modes[k * devices:(k + 1) * devices]
-
-    def exchange(source, target, sems):
-        def make(p):
-            peer = lax.rem(me + p, devices)
-            return pltpu.make_async_remote_copy(
-                src_ref=source.at[pl.ds(pl.multiple_of(peer * chunk, 8), chunk)],
-                dst_ref=target.at[pl.ds(pl.multiple_of(me * chunk, 8), chunk)],
-                send_sem=sems.at[0, p], recv_sem=sems.at[1, p],
-                device_id=where_is(peer), device_id_type=MESH)
-
-        def start(p, carry):
-            make(p).start()
-            return carry
-
-        def wait(p, carry):
-            make(p).wait()
-            return carry
-
-        lax.fori_loop(1, devices, start, 0)
-        own = pl.ds(pl.multiple_of(me * chunk, 8), chunk)
-        target[own, :] = source[own, :]
-        lax.fori_loop(1, devices, wait, 0)
-
-    exchange(s2, r2, sem2)
+                s2[c, pl.ds(z * jrows + k, devices, stride=chunk), :] = modes[k * devices:(k + 1) * devices]
+        send(s2, r2, sem2, c)
+
+    for c in range(3):
+        receive(s2, r2, sem2, c)
+        for k in range(kc):
+            omega[c, k] = turn(dot(both[...], r2[c, pl.ds(k, n, stride=jrows), :]), 1.0)
 
     xi = lax.broadcasted_iota(jnp.int32, (n, n), 1)
     zi = lax.broadcasted_iota(jnp.int32, (n, n), 0)
     kx = jnp.where(xi < half, xi, xi - half).astype(jnp.float32)
     kz = jnp.where(zi < half, zi, zi - n).astype(jnp.float32)
-    for k in range(kc):
-        yi = k * devices + me
-        ky_int = yi - jnp.where(yi < half, 0, n)
-        ky = jnp.full((n, n), ky_int, jnp.int32).astype(jnp.float32)
-        square = kx * kx + ky * ky + kz * kz
-        keep = (square > 0.0) & (zi != half) & (jnp.full((n, n), yi, jnp.int32) != half)
-        factor = jnp.where(keep, 1.0 / jnp.maximum(square, 1.0), 0.0) * (1.0 / (n * n * n))
-        ox, oy, oz = [turn(dot(both[...], r2[pl.ds(k * 3 + c, n, stride=jrows), :]), 1.0) for c in range(3)]
-        for c, cross in enumerate((ky * oz - kz * oy, kz * ox - kx * oz, kx * oy - ky * ox)):
-            hat = pltpu.roll(cross * factor, half, axis=1) * (-sign)
-            s3[pl.ds(k * 3 + c, n, stride=jrows), :] = turn(dot(both[...], hat), -1.0)
-
-    exchange(s3, r3, sem3)
-
-    for z in range(zc):
-        for c in range(3):
+    for c in range(3):
+        for k in range(kc):
+            yi = k * devices + me
+            ky_int = yi - jnp.where(yi < half, 0, n)
+            ky = jnp.full((n, n), ky_int, jnp.int32).astype(jnp.float32)
+            if c == 0:
+                square = kx * kx + ky * ky + kz * kz
+                keep = (square > 0.0) & (zi != half) & (jnp.full((n, n), yi, jnp.int32) != half)
+                factor[k] = jnp.where(keep, 1.0 / jnp.maximum(square, 1.0), 0.0) * (1.0 / (n * n * n))
+                cross = ky * omega[2, k] - kz * omega[1, k]
+            elif c == 1:
+                cross = kz * omega[0, k] - kx * omega[2, k]
+            else:
+                cross = kx * omega[1, k] - ky * omega[0, k]
+            hat = pltpu.roll(cross * factor[k], half, axis=1) * (-sign)
+            s3[c, pl.ds(k, n, stride=jrows), :] = turn(dot(both[...], hat), -1.0)
+        send(s3, r3, sem3, c)
+
+    def copy_back(c, p):
+        peer = lax.rem(row + p, rows)
+        return pltpu.make_async_remote_copy(
+            src_ref=w4.at[c, peer], dst_ref=r4.at[c, pl.ds(1 + row * zc, zc)], send_sem=sem4.at[0, c, p],
+            recv_sem=sem4.at[1, c, p], device_id=(peer, col), device_id_type=MESH)
+
+    def copy_layer(c, r, above):
+        step, side = (1, 0) if above else (cols - 1, 1)
+        return pltpu.make_async_remote_copy(
+            src_ref=w4.at[c, r, zc - 1 if above else 0], dst_ref=r4.at[c, 0 if above else nz + 1],
+            send_sem=sem4h.at[side, c, r], recv_sem=sem4h.at[side, c, rows],
+            device_id=(r, lax.rem(col + step, cols)), device_id_type=MESH)
+
+    for c in range(3):
+        receive(s3, r3, sem3, c)
+        for z in range(zc):
             modes = jnp.concatenate(
-                [r3[pl.ds(z * jrows + k * 3 + c, devices, stride=chunk), :] for k in range(kc)], axis=0)
+                [r3[c, pl.ds(z * jrows + k, devices, stride=chunk), :] for k in range(kc)], axis=0)
             lines = turn(dot(iy[...], modes), -1.0)
             for r in range(rows):
-                w4[r, z, pl.ds(c * padded, padded), :] = lines[r * padded:(r + 1) * padded]
-
-    def copy_back(p):
-        peer = lax.rem(row + p, rows)
-        return pltpu.make_async_remote_copy(
-            src_ref=w4.at[peer], dst_ref=r4.at[pl.ds(1 + row * zc, zc)], send_sem=sem4.at[0, p],
-            recv_sem=sem4.at[1, p], device_id=(peer, col), device_id_type=MESH)
-
-    def copy_layer(r, top):
-        step = 1 if top else cols - 1
-        return pltpu.make_async_remote_copy(
-            src_ref=w4.at[r, zc - 1 if top else 0], dst_ref=r4.at[0 if top else nz + 1],
-            send_sem=sem4h.at[0 if top else 1, r], recv_sem=sem4h.at[0 if top else 1, rows],
-            device_id=(r, lax.rem(col + step, cols)), device_id_type=MESH)
-
-    @pl.when(row == rows - 1)
-    def _():
-        for r in range(rows):
-            copy_layer(r, True).start()
-
-    @pl.when(row == 0)
-    def _():
-        for r in range(rows):
-            copy_layer(r, False).start()
-
-    last = [copy_back(p) for p in range(1, rows)]
-    for copy in last:
-        copy.start()
-    r4[pl.ds(1 + row * zc, zc)] = w4[row]
-    for copy in last:
-        copy.wait()
-    copy_layer(0, True).wait_recv()
-    copy_layer(0, False).wait_recv()
-
-    @pl.when(row == rows - 1)
-    def _():
-        for r in range(rows):
-            copy_layer(r, True).wait_send()
-
-    @pl.when(row == 0)
-    def _():
-        for r in range(rows):
-            copy_layer(r, False).wait_send()
+                w4[c, r, z] = lines[r * padded:(r + 1) * padded]
+
+        for p in range(1, rows):
+            copy_back(c, p).start()
+
+        @pl.when(row == rows - 1)
+        def _():
+            for r in range(rows):
+                copy_layer(c, r, True).start()
+
+        @pl.when(row == 0)
+        def _():
+            for r in range(rows):
+                copy_layer(c, r, False).start()
+
+        r4[c, pl.ds(1 + row * zc, zc)] = w4[c, row]
 
     top = jnp.zeros((8, n), jnp.float32)
-    for z in range(nz + 2):
-        product = dot(r4[z], bx[...])
-        size = jnp.abs(product[:, 2 * n:])
-        top = jnp.maximum(top, jnp.max(size.reshape(size.shape[0] // 8, 8, n), axis=0))
-        for c in range(3):
+    for c in range(3):
+        for p in range(1, rows):
+            copy_back(c, p).wait()
+        copy_layer(c, 0, True).wait_recv()
+        copy_layer(c, 0, False).wait_recv()
+        for z in range(nz + 2):
+            product = dot(r4[c, z], bx[...])
+            size = jnp.abs(product[:, 2 * n:])
+            top = jnp.maximum(top, jnp.max(size.reshape(size.shape[0] // 8, 8, n), axis=0))
             for h in range(2):
-                part = product[c * padded:(c + 1) * padded, h * n:(h + 1) * n]
+                part = product[:, h * n:(h + 1) * n]
                 fine[c * 2 + h, pl.ds(zp + z, ny, stride=zp), :] = part[:ny]
                 fine[c * 2 + h, pl.ds(z, 1), :] = part[ny:ny + 1]
                 fine[c * 2 + h, pl.ds((ny + 1) * zp + z, 1), :] = part[ny + 1:ny + 2]
+
+    @pl.when(row == rows - 1)
+    def _():
+        for c in range(3):
+            for r in range(rows):
+                copy_layer(c, r, True).wait_send()
+
+    @pl.when(row == 0)
+    def _():
+        for c in range(3):
+            for r in range(rows):
+                copy_layer(c, r, False).wait_send()
+
     peaks[me] = top
 
     def send_peak(p):
@@ -387,7 +399,7 @@
     ny, nz = vorticity.shape[1], vorticity.shape[2]
     devices = rows * cols
     zc, kc = nz // rows, n // devices
-    jrows = kc * 3
+    jrows = kc
     while zc * jrows % 8:
         jrows += 1
     padded = ny + 8
@@ -404,14 +416,16 @@
         out_specs=vmem,
         scratch_shapes=[
             pltpu.VMEM((3, ny * nz, n), f32),
-            pltpu.VMEM((rows, zc * 3 * ny, n), f32),
-            pltpu.VMEM((rows, zc * 3 * ny, n), f32),
-            pltpu.VMEM((total, n), f32),
-            pltpu.VMEM((total, n), f32),
-            pltpu.VMEM((total, n), f32),
-            pltpu.VMEM((total, n), f32),
-            pltpu.VMEM((rows, zc, 3 * padded, n), f32),
-            pltpu.VMEM((nz + 2, 3 * padded, n), f32),
+            pltpu.VMEM((3, rows, zc * ny, n), f32),
+            pltpu.VMEM((3, rows, zc * ny, n), f32),
+            pltpu.VMEM((3, total, n), f32),
+            pltpu.VMEM((3, total, n), f32),
+            pltpu.VMEM((3, kc, n, n), f32),
+            pltpu.VMEM((kc, n, n), f32),
+            pltpu.VMEM((3, total, n), f32),
+            pltpu.VMEM((3, total, n), f32),
+            pltpu.VMEM((3, rows, zc, padded, n), f32),
+            pltpu.VMEM((3, nz + 2, padded, n), f32),
             pltpu.VMEM((6, (ny + 2) * zp, n), f32),
             pltpu.VMEM((devices, 8, n), f32),
             pltpu.VMEM((12, nzf, n), f32),
@@ -422,11 +436,11 @@
             pltpu.VMEM((ny, 8, 2 * n), f32),
             pltpu.VMEM((ny, 8, 2 * n), f32),
             pltpu.VMEM((ny, 8, 2 * n), f32),
-            dma((2, rows)),
-            dma((2, devices)),
-            dma((2, devices)),
-            dma((2, rows)),
-            dma((2, rows + 1)),
+            dma((2, 3, rows)),
+            dma((2, 3, devices)),
+            dma((2, 3, devices)),
+            dma((2, 3, rows)),
+            dma((2, 3, rows + 1)),
             dma((2, devices)),
             dma((2, 2)),
             dma((2, 2, 3)),

time: 117 us -> 102 us (0.87)
  Pallas kernels: 114 us -> 98.3 us
    pallas_call x1, Pallas kernels: 114 us -> 98.3 us  [shards(): pl.pallas_call(functools.partial(body, rows, cols, jrows), out_shape=jax....]
where the time goes in v2:
time: 102 us; the launch traced here: 101 us
  Pallas kernels  98.3 us (96%)
  local copies, waits for them, and re-layouts  3.16 us (3%)
    pallas_call x1, Pallas kernels, shards(): pl.pallas_call(functools.partial(body, rows, cols, jrows), out_shape=jax....  98.3 us
    unnamed x1, local copies, waits for them, and re-layouts  3.16 us

profile of v2, /device:TPU:0, one launch (start us, length us, event | category | flops | bytes accessed | tf_op | source)
XLA Modules:
  0.0 101.4 jit_solution(10160785246892588590)
XLA Ops:
  0.0 98.3 %shard_map.64 = f32[64,32,256]{2,1,0:T(8,128)} custom-call(f32[3,512,128]{2,1,0:T(8,128)} %bitcast.1, f32[64,32,256]{2,1,0:T(8,128)} %scalar.1, f32[128,128]{1,0:T(8,128)} %constant.8.clone.fx, f32[256,128]{1,0:T(8,128)} %constant.9.clone.both, f32[320,128]{1,0:T(8,128)} %constant.10.clone.iy, f32[128,384]{1,0:T(8,128)} %constant.11.clone.bx), custom_call_target="tpu_custom_call" | custom-call | tf_op jit(solution)/shard_map/pallas_call | solution.py:412
  98.3 3.2 %copy.8 = f32[64,32,256]{2,1,0:T(8,128)} copy(f32[64,32,256]{2,1,0:T(8,128)} %shard_map.64) | data formatting | bytes 4194304
